TPU v7x, 256 devices: a whole 4x4x8 slice. The times are simulated.
256 devices in a mesh: dp: 16 (over y_lo, z), tp: 16 (over y_hi, x, core).
Axes of the slice: x: 4, y: 4 (y_hi: 2, y_lo: 2; y = y_hi * 2 + y_lo), z: 8, core: 2. Of those that a mesh axis runs over, the one named last changes fastest.
Arguments:
- queries: bfloat16 [512, 16, 8192], P(('dp', 'tp')), parts along dimension 0, may hold values from -512 to 512
- kv_cache: bfloat16 [512, 8, 384, 256], P(('dp', 'tp')), parts along dimension 0, may hold values from -18 to 18
- lengths: int32 [512], P(('dp', 'tp')), parts along dimension 0, may hold values from 17 to 384, as said below
- residual: bfloat16 [512, 16, 8192], P(('dp', 'tp')), parts along dimension 0, may hold values from -4 to 4
- out_weight: bfloat16 [8192, 8192], P('tp'), may hold values from -0.0625 to 0.0625
- norm_gain: bfloat16 [8192], replicated, may hold values from 0.25 to 1.75
Outputs:
- hidden: bfloat16 [512, 16, 8192], P(('dp', 'tp')), parts along dimension 0
- normed: bfloat16 [512, 16, 8192], P(('dp', 'tp')), parts along dimension 0
There are 16 independent parts, one for each index of `dp`. A program takes and returns all parts, laid end to end along the dimension named above; an argument that names none is the same for every part. Nothing has to cross between parts.
Inputs may be any that keep to these rules, and one draw needn't show every extreme that they name: `lengths`: some sequence of every part has exactly 384 live slots.
All inputs are finite; a program needn't handle non-finite values.
Results may differ from a plain program's by a relative error of at most 0.015.
Values may be sent and summed in bfloat16 or wider, within the bound.
A program may use at most 128 MiB of HBM per device.

v0:
```python
import jax
import jax.numpy as jnp
from jax import lax
from jax.sharding import Mesh
from jax.sharding import PartitionSpec as P

HEADS = 64
KV_HEADS = 8
HEAD_DIM = 128
DRAFT = 16
LEN = 384
TP = ("tp_0", "tp_1", "tp_2")
DP_TP = ("dp", "tp_0", "tp_1", "tp_2")


def split_up(shard, dim, length):
    before, after = (shard.shape[:dim], shard.shape[dim + 1 :])
    return jnp.moveaxis(shard.reshape(*before, length, -1, *after), dim, 0)


def laid_out(tiles, dim):
    shape = list(tiles.shape[1:])
    shape[dim] *= tiles.shape[0]
    return jnp.moveaxis(tiles, 0, dim).reshape(shape)


def turned_blocks(tiles, axes, turns):
    shape = [lax.axis_size(a) for a in axes]
    tiles = tiles.reshape(*shape, *tiles.shape[1:])
    for k in turns:
        tiles = lax.all_to_all(tiles, axes[k], split_axis=k, concat_axis=k, tiled=True)
    return tiles.reshape(-1, *tiles.shape[len(axes) :])


def core_and_chips(shard, groups, turns, split_dim, concat_dim):
    length = lax.axis_size(groups[0]) * lax.axis_size(groups[1])
    tiles = split_up(shard, split_dim, length)
    return laid_out(turned_blocks(tiles, groups, turns), concat_dim)


def attend(queries, kv_cache, lengths):
    seq_count = queries.shape[0]
    per_group = HEADS // KV_HEADS
    grouped = queries.reshape(seq_count, DRAFT, KV_HEADS, per_group, HEAD_DIM).transpose(
        0, 2, 3, 1, 4
    )
    grouped = grouped.reshape(seq_count, KV_HEADS, per_group * DRAFT, HEAD_DIM)
    key_part = kv_cache[..., :HEAD_DIM]
    value_part = kv_cache[..., HEAD_DIM:]
    scores = jnp.einsum(
        "skqd,skld->skql", grouped, key_part, preferred_element_type=jnp.float32
    ) * HEAD_DIM ** (-0.5)
    draft_index = jnp.arange(per_group * DRAFT, dtype=jnp.int32) % DRAFT
    visible = lengths[:, None, None, None] - DRAFT + 1 + draft_index[None, None, :, None]
    position = jnp.arange(LEN, dtype=jnp.int32)
    allowed = position[None, None, None, :] < visible
    scores = jnp.where(allowed, scores, -1e30)
    peak = jnp.max(scores, axis=-1, keepdims=True)
    raised = jnp.exp(scores - peak)
    totals = jnp.sum(raised, axis=-1, keepdims=True)
    weights = (raised / totals).astype(jnp.bfloat16)
    attended = jnp.einsum(
        "skql,skld->skqd", weights, value_part, preferred_element_type=jnp.float32
    ).astype(jnp.bfloat16)
    attended = attended.reshape(seq_count, KV_HEADS, per_group, DRAFT, HEAD_DIM).transpose(
        0, 3, 1, 2, 4
    )
    return attended.reshape(seq_count, DRAFT, HEADS * HEAD_DIM)


def on_device(queries, kv_cache, lengths, residual, out_weight, norm_gain):
    attended = attend(queries, kv_cache, lengths)
    by_heads = core_and_chips(attended, (("tp_0", "tp_1"), "tp_2"), (1, 0), 2, 0)
    flat_rows = by_heads.reshape(-1, by_heads.shape[2])
    own_rows = lax.psum_scatter(
        jnp.dot(flat_rows, out_weight, preferred_element_type=jnp.float32).astype(jnp.bfloat16),
        TP,
        scatter_dimension=0,
        tiled=True,
    ).astype(jnp.float32)
    summed = residual.astype(jnp.float32) + own_rows.reshape(residual.shape)
    hidden = summed.astype(jnp.bfloat16)
    scales = lax.rsqrt(jnp.mean(summed * summed, axis=-1, keepdims=True) + 1e-05)
    normed = (summed * scales * norm_gain.astype(jnp.float32)).astype(jnp.bfloat16)
    return (hidden, normed)


def solution(mesh):
    finer = Mesh(mesh.devices.reshape(mesh.shape["dp"], 2, 4, 2), ("dp", "tp_0", "tp_1", "tp_2"))
    placed = (
        P(DP_TP, None, None),
        P(DP_TP, None, None, None),
        P(DP_TP),
        P(DP_TP, None, None),
        P(TP, None),
        P(),
    )
    return jax.shard_map(
        on_device,
        mesh=finer,
        in_specs=placed,
        out_specs=(P(DP_TP, None, None), P(DP_TP, None, None)),
        check_vma=False,
    )
```

profile of v0, /device:TPU:192, one launch (start us, length us, event | category | flops | bytes accessed | tf_op | source)
XLA Modules:
  0.0 165.4 jit_solution(15635852313200560224)
XLA Ops:
  7.2 0.0 reduce-scatter.2.cloned.1.call-start
  7.2 1.2 copy.16
  8.4 0.3 copy.12
  8.7 0.7 broadcast_add_fusion.1
  9.4 0.1 broadcast_add_fusion
  9.5 0.1 iota_compare_fusion
  9.6 2.2 %fusion.6 = f32[2,8,128,384]{3,2,1,0:T(8,128)S(1)} fusion(bf16[2,8,128,128]{3,2,1,0:T(8,128)(2,1)S(1)} %bitcast.26, bf16[2,8,384,256]{3,2,1,0:T(8,128)(2,1)} %param.7), kind=kOutput, calls=%fused_computation.10 | convolution fusion | flops 201326592 | bytes 5242880 | tf_op jit(solution)/shard_map/skqd,skld->skql/dot_general | solution.py:50
  11.8 0.0 copy-start.1
  11.8 1.6 fusion.15
  13.4 0.3 copy-done.1
  13.7 0.6 fusion.9
  14.3 0.1 copy.18
  14.5 0.3 reshape_reshape.3
  14.8 0.2 reshape.86
  15.0 0.3 copy.14
  15.3 4.2 %all_to_all.10 = bf16[8,2,2,16,512]{4,3,2,0,1:T(8,128)(2,1)S(1)} all-to-all(bf16[8,2,2,16,512]{4,3,2,0,1:T(8,128)(2,1)S(1)} %copy.14), channel_id=1, replica_groups=mesh['dp'=16,'tp_0'=2,'tp_1'=4,'tp_2'=2] {'tp_2'}, dimensions={1} | all-to-all | bytes 1048576 | tf_op jit(solution)/shard_map/all_to_all | solution.py:31
  19.5 18.6 %all_to_all.11 = bf16[8,2,2,16,512]{4,3,2,1,0:T(8,128)(2,1)S(1)} all-to-all(bf16[8,2,2,16,512]{4,3,2,1,0:T(8,128)(2,1)S(1)} %copy.15), channel_id=1, replica_groups=mesh['dp'=16,'tp_0'=2,'tp_1'=4,'tp_2'=2] {'tp_0','tp_1'}, dimensions={0} | all-to-all | bytes 1048576 | tf_op jit(solution)/shard_map/all_to_all | solution.py:31
  38.1 10.1 %convolution_convert_fusion = bf16[512,8192]{1,0:T(8,128)(2,1)} fusion(bf16[512,512]{1,0:T(8,128)(2,1)S(1)} %bitcast.33, bf16[512,8192]{1,0:T(8,128)(2,1)} %param.10), kind=kOutput, calls=%fused_computation.1 | convolution fusion | flops 4299161600 | bytes 17301504 | tf_op jit(solution)/shard_map/dot_general | solution.py:76
  48.2 0.0 copy-start.2
  48.2 0.0 copy-start
  48.2 0.0 reduce-scatter.2.cloned.1.call-update
  48.2 0.7 copy-done.2
  48.9 106.1 %reduce-scatter.2.cloned.1.call-done = bf16[32,8192]{1,0:T(8,128)(2,1)} async-done(((bf16[512,8192]{1,0:T(8,128)(2,1)}), bf16[32,8192]{1,0:T(8,128)(2,1)}) %reduce-scatter.2.cloned.1.call-update) | async-done | bytes 524304 | tf_op jit(solution)/shard_map/reduce_scatter | solution.py:75
  155.0 0.0 copy-done
  155.0 1.3 multiply_reduce_fusion
  156.3 2.2 %multiply_convert_fusion = (bf16[2,16,8192]{2,1,0:T(8,128)(2,1)}, bf16[2,16,8192]{2,1,0:T(8,128)(2,1)}) fusion(bf16[2,16,8192]{2,1,0:T(8,128)(2,1)S(1)} %copy-done, f32[8192]{0:T(1024)S(1)} %convert_element_type.27, f32[2,16]{1,0:T(2,128)S(1)} %add_rsqrt_fusion, bf16[32,8192]{1,0:T(8,128)(2,1)} %reduce-scatter.2.cloned.1.call-done), kind=kLoop, calls=%fused_computation.15 | loop fusion | flops 1835008 | bytes 2130048 | tf_op jit(solution)/shard_map/convert_element_type | solution.py:84
  (4 shorter events, 0.1 us)
Async XLA Ops:
  7.2 147.9 %reduce-scatter.2.cloned.1.call-start = ((), (), s32[]{:S(2)}) async-start(), calls=%async_computation.3 | async-start | bytes 8912896 | tf_op jit(solution)/shard_map/reduce_scatter | solution.py:75
  11.8 1.9 %copy-start.1 = (bf16[2,8,384,256]{3,2,1,0:T(8,128)(2,1)S(1)}, bf16[2,8,384,256]{3,2,1,0:T(8,128)(2,1)}, u32[]{:S(2)}) copy-start(bf16[2,8,384,256]{3,2,1,0:T(8,128)(2,1)} %param.7) | copy-start | bytes 9437188
  48.2 0.7 copy-start.2
  48.2 106.8 %copy-start = (bf16[2,16,8192]{2,1,0:T(8,128)(2,1)S(1)}, bf16[2,16,8192]{2,1,0:T(8,128)(2,1)}, u32[]{:S(2)}) copy-start(bf16[2,16,8192]{2,1,0:T(8,128)(2,1)} %param.9) | copy-start | bytes 1572868
Sparse Core Ops, SparseCore 0:
  48.3 106.6 reduce-scatter.1
where the time goes:
time: 168 us; the launch traced here: 165 us
  waiting for transfers between devices  106 us (63%)
  blocking collectives  22.8 us (14%)
  between operations  14.1 us (8%)
  matrix products  12.9 us (8%)
  other arithmetic  5.95 us (4%)
  local copies, waits for them, and re-layouts  3.51 us (2%)
    reduce_scatter x1, waiting for transfers between devices, on_device(): lax.psum_scatter(jnp.dot(flat_rows, out_weight, preferred_element_type=jn...  106 us
    all_to_all x2, blocking collectives, turned_blocks(): lax.all_to_all(tiles, axes[k], split_axis=k, concat_axis=k, tiled=True)  22.8 us
    dot_general x1, matrix products, on_device(): jnp.dot(flat_rows, out_weight, preferred_element_type=jnp.float32)  10.1 us
  transfers between devices with their start and end apart: 1, of which 1 were waited for; matrix products, arithmetic and copies ran while one was open for 0% of the time, Pallas kernels for 0%

commit v1 on v0

v1 whole, which is shorter than its diff:
```python
import functools

import jax
import jax.numpy as jnp
from jax import lax
from jax.experimental import pallas as pl
from jax.experimental.pallas import tpu as pltpu
from jax.sharding import PartitionSpec as P

KV_HEADS = 8
HEAD_DIM = 128
GROUP = 8
DRAFT = 16
TILE = 256
MESH = pl.DeviceIdType.MESH
F32 = jnp.float32
BF16 = jnp.bfloat16

CHUNKS = ((1, 2), (2, 2), (1, 2), (2, 2), (1, 2), (2, 2), (1, 3), (2, 1))

FAR_UP, FAR_DOWN, NEAR_UP, NEAR_DOWN, SUM_UP, SUM_DOWN, ACROSS = range(7)

ORDER = (
    ("d", 0), ("d", 2), ("s", 1), ("d", 4), ("z", 0), ("d", 1), ("s", 3), ("d", 6),
    ("z", 2), ("d", 3), ("s", 5), ("z", 4), ("f", 1), ("d", 5), ("s", 7), ("f", 0),
    ("z", 6), ("d", 7), ("f", 3), ("f", 2), ("f", 5), ("f", 4), ("f", 7), ("f", 6),
)


def kernel(
    dp_half,
    lengths,
    q_hbm,
    kv_hbm,
    res_hbm,
    w_hbm,
    gain,
    hid_hbm,
    norm_hbm,
    q,
    kv,
    res,
    w,
    stage,
    att,
    part,
    far_up,
    far_down,
    from_down,
    from_up,
    across,
    total,
    hid,
    norm,
    in_sem,
    kv_sem,
    w_sem,
    swap_send,
    swap_recv,
    a_send,
    a_recv,
    r_send,
    r_recv,
    out_sem,
):
    seqs = q.shape[0]
    rows = seqs * DRAFT
    width = part.shape[3]
    dp, tp = lax.axis_index("dp"), lax.axis_index("tp")
    y_hi, x, core = tp // 8, (tp // 2) % 4, tp % 2

    def peer(dx, dy):
        return (
            (dp + dy * dp_half) % (2 * dp_half),
            ((y_hi + dy) % 2) * 8 + ((x + dx) % 4) * 2 + core,
        )

    sibling = (dp, tp + 1 - 2 * core)

    def turn(i):
        h = i // 2
        return (2 - h * (h + 1) // 2) % 4, (i + 1) % 2

    chunks, start = [], 0
    for kind, share in CHUNKS:
        size = share * width // 16
        chunks.append((kind, start, size))
        start += size

    q_copy = pltpu.make_async_copy(q_hbm, q, in_sem.at[0])
    q_copy.start()

    def kv_head(i):
        dx, dy = turn(i)
        return ((y_hi + dy) % 2) * 4 + (x + dx) % 4

    def kv_copy(i):
        return pltpu.make_async_copy(kv_hbm.at[:, kv_head(i)], kv.at[i], kv_sem.at[i])

    for i in range(KV_HEADS):
        kv_copy(i).start()

    barrier = pltpu.get_barrier_semaphore()
    friends = [sibling] + [peer(i % 4, i // 4) for i in range(1, 8)]
    for friend in friends:
        pl.semaphore_signal(barrier, inc=1, device_id=friend, device_id_type=MESH)

    res_copy = pltpu.make_async_copy(res_hbm, res, in_sem.at[1])
    res_copy.start()

    def w_copy(j):
        cols = pl.ds(chunks[j][1], chunks[j][2])
        return pltpu.make_async_copy(w_hbm.at[:, cols], w.at[0, :, cols], w_sem.at[j])

    def swap_copy(j):
        cols = pl.ds(chunks[j][1], chunks[j][2])
        return pltpu.make_async_remote_copy(
            w_hbm.at[:, cols],
            w.at[1, :, cols],
            swap_send.at[j],
            swap_recv.at[j],
            device_id=sibling,
            device_id_type=MESH,
        )

    pl.semaphore_wait(barrier, len(friends))
    for j in range(len(chunks)):
        swap_copy(j).start()
    for j in range(len(chunks)):
        w_copy(j).start()

    def att_copy(i):
        dx, dy = turn(i)
        return pltpu.make_async_remote_copy(
            stage.at[i],
            att.at[dy, (4 - dx) % 4],
            a_send.at[i],
            a_recv.at[i],
            device_id=peer(dx, dy),
            device_id_type=MESH,
        )

    draft = lax.broadcasted_iota(jnp.int32, (GROUP * DRAFT, kv.shape[2]), 0) % DRAFT
    slot = lax.broadcasted_iota(jnp.int32, (GROUP * DRAFT, kv.shape[2]), 1)
    ahead = slot - draft
    q_copy.wait()

    def one_head(i, carry):
        k = kv_head(i)
        kv_copy(i).wait()
        cols = pl.ds(pl.multiple_of(k * GROUP * HEAD_DIM, GROUP * HEAD_DIM), GROUP * HEAD_DIM)
        for s in range(seqs):
            heads = q[s, :, cols]
            grouped = jnp.concatenate(
                [heads[:, g * HEAD_DIM : (g + 1) * HEAD_DIM] for g in range(GROUP)], axis=0
            )
            keys = kv[i, s, :, :HEAD_DIM]
            values = kv[i, s, :, HEAD_DIM:]
            scores = lax.dot_general(
                grouped, keys, (((1,), (1,)), ((), ())), preferred_element_type=F32
            ) * (HEAD_DIM ** (-0.5))
            scores = jnp.where(ahead < lengths[s] - DRAFT + 1, scores, -1e30)
            peak = jnp.max(scores, axis=-1, keepdims=True)
            raised = jnp.exp(scores - peak)
            sums = jnp.sum(raised, axis=-1, keepdims=True)
            out = jnp.dot(raised.astype(BF16), values, preferred_element_type=F32)
            out = (out / sums).astype(BF16)
            stage[i, s * DRAFT : (s + 1) * DRAFT, :] = jnp.concatenate(
                [out[g * DRAFT : (g + 1) * DRAFT] for g in range(GROUP)], axis=1
            )

        @pl.when(i < KV_HEADS - 1)
        def _():
            att_copy(i).start()

        return carry

    lax.fori_loop(0, KV_HEADS, one_head, 0)
    att[0, 0] = stage[KV_HEADS - 1]

    def remote(j, which, source, target, device):
        return pltpu.make_async_remote_copy(
            source,
            target,
            r_send.at[j, which],
            r_recv.at[j, which],
            device_id=device,
            device_id_type=MESH,
        )

    low, high = pl.ds(0, rows // 2), pl.ds(rows // 2, rows // 2)
    up, down, over = peer(1, 0), peer(3, 0), peer(0, 1)

    def copies(j):
        kind, begin, size = chunks[j]
        cols = pl.ds(begin, size)
        if kind == 1:
            pairs = {
                FAR_UP: (part.at[0, 2, :, cols], far_up.at[:, cols], up),
                FAR_DOWN: (part.at[1, 2, :, cols], far_down.at[:, cols], down),
                NEAR_UP: (part.at[1, 1, :, cols], from_down.at[1, :, cols], up),
                NEAR_DOWN: (part.at[0, 3, :, cols], from_up.at[0, :, cols], down),
                SUM_UP: (part.at[0, 1, :, cols], from_down.at[0, :, cols], up),
                SUM_DOWN: (part.at[1, 3, :, cols], from_up.at[1, :, cols], down),
                ACROSS: (part.at[1, 0, :, cols], across.at[0, :, cols], over),
            }
        else:
            pairs = {
                FAR_UP: (part.at[0, 2, low, cols], far_up.at[low, cols], up),
                FAR_DOWN: (part.at[0, 2, high, cols], far_down.at[high, cols], down),
                NEAR_UP: (part.at[0, 1, high, cols], from_down.at[0, high, cols], up),
                NEAR_DOWN: (part.at[0, 3, low, cols], from_up.at[0, low, cols], down),
                SUM_UP: (part.at[0, 1, low, cols], from_down.at[0, low, cols], up),
                SUM_DOWN: (part.at[0, 3, high, cols], from_up.at[0, high, cols], down),
                ACROSS: (part.at[1, :, :, cols], across.at[:, :, cols], over),
            }
        return {which: remote(j, which, *pair) for which, pair in pairs.items()}

    for i in range(KV_HEADS - 1):
        att_copy(i).wait_recv()
    for j, (kind, begin, size) in enumerate(chunks):
        w_copy(j).wait()
        swap_copy(j).wait_recv()

        def tile(n, carry, begin=begin):
            cols = pl.ds(pl.multiple_of(begin + n * TILE, TILE), TILE)
            half = w.shape[1]
            own = pl.ds(pl.multiple_of(core * half, half), half)
            other = pl.ds(pl.multiple_of((1 - core) * half, half), half)
            count = 8 * rows
            out = jnp.dot(
                att[:, :, :, own].reshape(count, half), w[0, :, cols], preferred_element_type=F32
            ) + jnp.dot(
                att[:, :, :, other].reshape(count, half), w[1, :, cols], preferred_element_type=F32
            )
            part[:, :, :, cols] = out.astype(BF16).reshape(2, 4, rows, TILE)
            return carry

        lax.fori_loop(0, size // TILE, tile, 0)
        sends = copies(j)
        first = (FAR_UP, FAR_DOWN, NEAR_UP, NEAR_DOWN) if kind == 1 else (ACROSS,)
        for which in first:
            sends[which].start()

    def add(target, *terms):
        value = part[target].astype(F32)
        for ref, index in terms:
            value = value + ref[index].astype(F32)
        part[target] = value.astype(BF16)

    every = slice(None)
    top, bottom = slice(0, rows // 2), slice(rows // 2, rows)
    res_copy.wait()
    squares = []

    def hidden_copy(j):
        cols = pl.ds(chunks[j][1], chunks[j][2])
        return pltpu.make_async_copy(hid.at[:, :, cols], hid_hbm.at[:, :, cols], out_sem.at[j])

    for step, j in ORDER:
        kind, begin, size = chunks[j]
        cols = slice(begin, begin + size)
        sends = copies(j)
        if step == "s":
            sends[ACROSS].wait_recv()
            for dx in (2, 1, 3):
                add((0, dx, every, cols), (across, (dx, every, cols)))
            for which in (FAR_UP, FAR_DOWN, NEAR_UP, NEAR_DOWN):
                sends[which].start()
        elif step == "d":
            sends[FAR_UP].wait_recv()
            lines = every if kind == 1 else top
            add((0, 1, lines, cols), (far_up, (lines, cols)))
            sends[SUM_UP].start()
            sends[FAR_DOWN].wait_recv()
            lines = every if kind == 1 else bottom
            add((1 if kind == 1 else 0, 3, lines, cols), (far_down, (lines, cols)))
            sends[SUM_DOWN].start()
        elif step == "z":
            for which in (NEAR_UP, NEAR_DOWN, SUM_UP, SUM_DOWN):
                sends[which].wait_recv()
            add(
                (1, 0, every, cols),
                (from_down, (1, every, cols)),
                (from_up, (1, every, cols)),
            )
            sends[ACROSS].start()
        else:
            if kind == 1:
                sends[ACROSS].wait_recv()
            else:
                for which in (NEAR_UP, NEAR_DOWN, SUM_UP, SUM_DOWN):
                    sends[which].wait_recv()
            value = (
                part[0, 0, :, cols].astype(F32)
                + from_down[0, :, cols].astype(F32)
                + from_up[0, :, cols].astype(F32)
                + across[0, :, cols].astype(F32)
                + res[:, :, cols].astype(F32).reshape(rows, size)
            )
            total[:, cols] = value
            hid[:, :, cols] = value.astype(BF16).reshape(seqs, DRAFT, size)
            hidden_copy(j).start()
            squares.append(jnp.sum(value * value, axis=-1, keepdims=True))

    scale = lax.rsqrt(sum(squares) / width + 1e-5)
    for j, (kind, begin, size) in enumerate(chunks):
        cols = slice(begin, begin + size)
        value = total[:, cols] * scale * gain[:, cols].astype(F32)
        norm[:, :, cols] = value.astype(BF16).reshape(seqs, DRAFT, size)
    norm_copy = pltpu.make_async_copy(norm, norm_hbm, in_sem.at[2])
    norm_copy.start()

    for i in range(KV_HEADS - 1):
        att_copy(i).wait_send()
    for j in range(len(chunks)):
        swap_copy(j).wait_send()
        for copy in copies(j).values():
            copy.wait_send()
        hidden_copy(j).wait()
    norm_copy.wait()


def solution(mesh):
    dp_half = mesh.shape["dp"] // 2

    def on_device(queries, kv_cache, lengths, residual, out_weight, norm_gain):
        seqs = queries.shape[0]
        rows = seqs * DRAFT
        depth, width = out_weight.shape
        slots = kv_cache.shape[2]
        n = len(CHUNKS)
        anywhere = pl.BlockSpec(memory_space=pl.ANY)
        dma = pltpu.SemaphoreType.DMA
        return pl.pallas_call(
            functools.partial(kernel, dp_half),
            out_shape=(jax.ShapeDtypeStruct((seqs, DRAFT, width), BF16),) * 2,
            in_specs=[pl.BlockSpec(memory_space=pltpu.SMEM)]
            + [anywhere] * 4
            + [pl.BlockSpec(memory_space=pltpu.VMEM)],
            out_specs=(anywhere, anywhere),
            scratch_shapes=[
                pltpu.VMEM(queries.shape, BF16),
                pltpu.VMEM((KV_HEADS, seqs, slots, 2 * HEAD_DIM), BF16),
                pltpu.VMEM(residual.shape, BF16),
                pltpu.VMEM((2, depth, width), BF16),
                pltpu.VMEM((KV_HEADS, rows, GROUP * HEAD_DIM), BF16),
                pltpu.VMEM((2, 4, rows, GROUP * HEAD_DIM), BF16),
                pltpu.VMEM((2, 4, rows, width), BF16),
                pltpu.VMEM((rows, width), BF16),
                pltpu.VMEM((rows, width), BF16),
                pltpu.VMEM((2, rows, width), BF16),
                pltpu.VMEM((2, rows, width), BF16),
                pltpu.VMEM((4, rows, width), BF16),
                pltpu.VMEM((rows, width), F32),
                pltpu.VMEM(residual.shape, BF16),
                pltpu.VMEM(residual.shape, BF16),
                dma((3,)),
                dma((KV_HEADS,)),
                dma((n,)),
                dma((n,)),
                dma((n,)),
                dma((KV_HEADS,)),
                dma((KV_HEADS,)),
                dma((n, 7)),
                dma((n, 7)),
                dma((n,)),
            ],
            compiler_params=pltpu.CompilerParams(
                collective_id=0, has_side_effects=True, vmem_limit_bytes=56 * 1024 * 1024
            ),
        )(lengths, queries, kv_cache, residual, out_weight, norm_gain.reshape(1, -1))

    seq = P(("dp", "tp"))
    return jax.shard_map(
        on_device,
        mesh=mesh,
        in_specs=(seq, seq, seq, seq, P("tp"), P()),
        out_specs=(seq, seq),
        check_vma=False,
    )
```

time: 168 us -> 58.8 us (0.35); the launches traced: 165 us -> 58.5 us
  waiting for transfers between devices: 106 us -> 0 us
  Pallas kernels: 0 us -> 52.8 us
  blocking collectives: 22.8 us -> 0 us
  between operations: 14.1 us -> 0.64 us
  matrix products: 12.9 us -> 0 us
  other arithmetic: 5.95 us -> 0 us
    reduce_scatter x1 -> x0, waiting for transfers between devices: 106 us -> none  [on_device(): lax.psum_scatter(jnp.dot(flat_rows, out_weight, preferred_element_type=jn...]
    pallas_call x0 -> x1, Pallas kernels: none -> 52.8 us  [on_device(): pl.pallas_call(functools.partial(kernel, dp_half), out_shape=(jax.ShapeDt...]
    all_to_all x2 -> x0, blocking collectives: 22.8 us -> none  [turned_blocks(): lax.all_to_all(tiles, axes[k], split_axis=k, concat_axis=k, tiled=True)]
    dot_general x3 -> x0, matrix products: 12.9 us -> none  [the longest x1 10.1 us: on_device(): jnp.dot(flat_rows, out_weight, preferred_element_type=jnp.float32)]
    convert_element_type x2 -> x0, other arithmetic: 2.22 us -> none  [the longest x1 2.22 us: on_device(): (summed * scales * norm_gain.astype(jnp.float32)).astype(jnp.bfloat16)]
    unnamed x7 -> x2, local copies, waits for them, and re-layouts: 2.18 us -> 3.74 us
  transfers between devices with their start and end apart: 1 -> 0, of which waited for: 1 -> 0; matrix products, arithmetic and copies ran while one was open for 0% -> 0% of each run, Pallas kernels for 0% -> 0%
where the time goes in v1:
time: 58.8 us; the launch traced here: 58.5 us
  Pallas kernels  52.8 us (90%)
  local copies, waits for them, and re-layouts  5.09 us (9%)
  between operations  0.64 us (1%)
    pallas_call x1, Pallas kernels, on_device(): pl.pallas_call(functools.partial(kernel, dp_half), out_shape=(jax.ShapeDt...  52.8 us
    unnamed x2, local copies, waits for them, and re-layouts  3.74 us
    reshape x1, local copies, waits for them, and re-layouts, on_device(): norm_gain.reshape(1, -1)  1.35 us

profile of v1, /device:TPU:192, one launch (start us, length us, event | category | flops | bytes accessed | tf_op | source)
XLA Modules:
  0.0 58.5 jit_solution(2923918468092415697)
XLA Ops:
  0.6 1.4 %reshape.7.gain = bf16[1,8192]{1,0:T(2,128)(2,1)} reshape(bf16[8192]{0:T(1024)(128)(2,1)} %param.11) | data formatting | bytes 32768 | tf_op jit(solution)/shard_map/reshape | solution.py:372
  2.0 52.8 %shard_map.77 = (bf16[2,16,8192]{2,1,0:T(8,128)(2,1)}, bf16[2,16,8192]{2,1,0:T(8,128)(2,1)}) custom-call(s32[2]{0:T(128)} %lengths.1, bf16[2,16,8192]{2,1,0:T(8,128)(2,1)} %q_hbm.1, bf16[2,8,384,256]{3,2,1,0:T(8,128)(2,1)} %kv_hbm.1, bf16[2,16,8192]{2,1,0:T(8,128)(2,1)} %res_hbm.1, bf16[512,8192]{1,0:T(8,128)(2,1)} %w_hbm.1, bf16[1,8192]{1,0:T(2,128)(2,1)} %reshape.7.gain), custom_call_target="tpu_custom_call" | custom-call | tf_op jit(solution)/shard_map/pallas_call | solution.py:335
  54.7 1.9 %copy.10 = bf16[2,16,8192]{2,1,0:T(8,128)(2,1)} copy(bf16[2,16,8192]{2,1,0:T(8,128)(2,1)} %get-tuple-element.4) | data formatting | bytes 1048576
  56.6 1.9 %copy.11 = bf16[2,16,8192]{2,1,0:T(8,128)(2,1)} copy(bf16[2,16,8192]{2,1,0:T(8,128)(2,1)} %get-tuple-element.5) | data formatting | bytes 1048576

commit v2 on v0

v2 whole, which is shorter than its diff:
```python
import functools

import jax
import jax.numpy as jnp
from jax import lax
from jax.experimental import pallas as pl
from jax.experimental.pallas import tpu as pltpu
from jax.sharding import PartitionSpec as P

KV_HEADS = 8
HEAD_DIM = 128
GROUP = 8
DRAFT = 16
TILE = 512
VMEM_LIMIT = 54735667
MESH = pl.DeviceIdType.MESH
F32 = jnp.float32
BF16 = jnp.bfloat16

CHUNKS = (
    (1, 0, 16, 0, 2),
    (2, 0, 16, 9, 2),
    (1, 16, 16, 0, 2),
    (2, 16, 16, 9, 2),
    (1, 0, 16, 2, 2),
    (1, 16, 16, 2, 2),
    (2, 0, 32, 11, 2),
    (1, 0, 32, 4, 2),
    (2, 0, 32, 13, 2),
    (1, 0, 32, 6, 2),
    (1, 0, 32, 8, 1),
    (2, 0, 32, 15, 1),
)
PIECES = ((0, 2), (9, 2), (2, 2), (11, 2), (4, 2), (13, 2), (6, 2), (15, 1), (8, 1))

FAR_UP, FAR_DOWN, NEAR_UP, NEAR_DOWN, SUM_UP, SUM_DOWN, ACROSS = range(7)

PLAN = (
    ("m", 0), ("x", 0), ("m", 1), ("y", 1), ("e", 0), ("m", 4), ("x", 4), ("e", 4), ("m", 3),
    ("y", 3), ("d", 0), ("m", 5), ("e", 5), ("x", 5), ("m", 2), ("e", 2), ("m", 6), ("s", 1),
    ("x", 2), ("y", 6), ("d", 4), ("m", 7), ("x", 7), ("e", 7), ("m", 8), ("y", 8), ("d", 5),
    ("z", 0), ("m", 9), ("x", 9), ("m", 11), ("y", 11), ("d", 7), ("e", 9), ("m", 10), ("d", 9),
    ("x", 10), ("d", 1), ("d", 2), ("s", 3), ("e", 1), ("e", 10), ("z", 7), ("z", 5), ("s", 6),
    ("d", 10), ("s", 8), ("e", 8), ("d", 3), ("z", 4), ("z", 9), ("s", 11), ("z", 2), ("f", 1),
    ("e", 3), ("e", 6), ("z", 10), ("d", 6), ("d", 8), ("e", 11), ("f", 5), ("d", 11), ("f", 9),
    ("f", 6), ("f", 7), ("f", 2), ("f", 4), ("f", 8), ("f", 3), ("f", 10), ("f", 0), ("f", 11),
)


def kernel(
    dp_half,
    lengths,
    q_hbm,
    kv_hbm,
    res_hbm,
    w_hbm,
    hid,
    total_0,
    total_1,
    scale,
    q,
    kv,
    res,
    w,
    stage,
    att,
    part,
    far_up,
    far_down,
    from_down,
    from_up,
    across,
    in_sem,
    q_sem,
    kv_sem,
    w_sem,
    swap_send,
    swap_recv,
    a_send,
    a_recv,
    r_send,
    r_recv,
):
    seqs = q.shape[0]
    width = part.shape[3]
    unit = width // 16
    dp, tp = lax.axis_index("dp"), lax.axis_index("tp")
    y_hi, x, core = tp // 8, (tp // 2) % 4, tp % 2

    def peer(dx, dy):
        return (
            (dp + dy * dp_half) % (2 * dp_half),
            ((y_hi + dy) % 2) * 8 + ((x + dx) % 4) * 2 + core,
        )

    sibling = (dp, tp + 1 - 2 * core)

    def turn(i):
        h = i % 4
        return (2 - h * (h + 1) // 2) % 4, 1 - i // 4

    def kv_head(i):
        dx, dy = turn(i)
        return ((y_hi + dy) % 2) * 4 + (x + dx) % 4

    def q_copy(s, i):
        wide = GROUP * HEAD_DIM
        cols = pl.ds(pl.multiple_of(kv_head(i) * wide, wide), wide)
        return pltpu.make_async_copy(q_hbm.at[s, :, cols], q.at[s, i], q_sem.at[s, i])

    def kv_copy(s, i):
        return pltpu.make_async_copy(kv_hbm.at[s, kv_head(i)], kv.at[s, i], kv_sem.at[s, i])

    def w_copy(j):
        cols = pl.ds(PIECES[j][0] * unit, PIECES[j][1] * unit)
        return pltpu.make_async_copy(w_hbm.at[:, cols], w.at[0, :, cols], w_sem.at[j])

    def swap_copy(j):
        cols = pl.ds(PIECES[j][0] * unit, PIECES[j][1] * unit)
        return pltpu.make_async_remote_copy(
            w_hbm.at[:, cols],
            w.at[1, :, cols],
            swap_send.at[j],
            swap_recv.at[j],
            device_id=sibling,
            device_id_type=MESH,
        )

    barrier = pltpu.get_barrier_semaphore()
    friends = [sibling] + [peer(i % 4, i // 4) for i in range(1, 8)]
    for friend in friends:
        pl.semaphore_signal(barrier, inc=1, device_id=friend, device_id_type=MESH)
    for i in range(KV_HEADS):
        q_copy(0, i).start()
        kv_copy(0, i).start()
    res_copy = pltpu.make_async_copy(res_hbm, res, in_sem.at[0])

    def att_copy(s, i):
        dx, dy = turn(i)
        return pltpu.make_async_remote_copy(
            stage.at[s, i],
            att.at[dy, (4 - dx) % 4, pl.ds(s * DRAFT, DRAFT)],
            a_send.at[s, i],
            a_recv.at[s, i],
            device_id=peer(dx, dy),
            device_id_type=MESH,
        )

    slots = kv.shape[3 - 1]
    draft = lax.broadcasted_iota(jnp.int32, (GROUP * DRAFT, slots), 0) % DRAFT
    slot = lax.broadcasted_iota(jnp.int32, (GROUP * DRAFT, slots), 1)
    ahead = slot - draft

    def attend(s, heads):
        for i in heads:
            q_copy(s, i).wait()
            kv_copy(s, i).wait()
        for i in heads:
            own = q[s, i]
            grouped = jnp.concatenate(
                [own[:, g * HEAD_DIM : (g + 1) * HEAD_DIM] for g in range(GROUP)], axis=0
            )
            keys = kv[s, i, :, :HEAD_DIM]
            values = kv[s, i, :, HEAD_DIM:]
            scores = lax.dot_general(
                grouped, keys, (((1,), (1,)), ((), ())), preferred_element_type=F32
            ) * (HEAD_DIM ** (-0.5))
            scores = jnp.where(ahead < lengths[s] - DRAFT + 1, scores, -1e30)
            raised = jnp.exp(scores - jnp.max(scores, axis=-1, keepdims=True))
            sums = jnp.sum(raised, axis=-1, keepdims=True)
            out = jnp.dot(raised.astype(BF16), values, preferred_element_type=F32)
            out = (out / sums).astype(BF16)
            stage[s, i] = jnp.concatenate(
                [out[g * DRAFT : (g + 1) * DRAFT] for g in range(GROUP)], axis=1
            )

    def some_heads(s, count):
        def body(h, carry):
            heads = [count * h + n for n in range(count)]
            attend(s, heads)
            for n in range(count - 1):
                att_copy(s, heads[n]).start()

            @pl.when(h < KV_HEADS // count - 1)
            def _():
                att_copy(s, heads[count - 1]).start()

            return carry

        return body

    with jax.named_scope("heads#s=0a"):
        attend(0, (0, 1))
    for s in range(1, seqs):
        for i in range(KV_HEADS):
            q_copy(s, i).start()
            kv_copy(s, i).start()
    with jax.named_scope("barrier"):
        pl.semaphore_wait(barrier, len(friends))
    for i in (0, 1):
        att_copy(0, i).start()
    for j in range(len(PIECES)):
        swap_copy(j).start()
        w_copy(j).start()
    res_copy.start()
    with jax.named_scope("heads#s=0"):
        lax.fori_loop(1, KV_HEADS // 2, some_heads(0, 2), 0)
    for s in range(1, seqs):
        with jax.named_scope("heads#s=1"):
            lax.fori_loop(0, KV_HEADS // 4, some_heads(s, 4), 0)
    for s in range(seqs):
        att[0, 0, s * DRAFT : (s + 1) * DRAFT] = stage[s, KV_HEADS - 1]

    up, down, over = peer(1, 0), peer(3, 0), peer(0, 1)

    def area(c):
        kind, row, count, begin, size = CHUNKS[c]
        return kind, slice(row, row + count), slice(begin * unit, (begin + size) * unit)

    def halves(c):
        kind, row, count, begin, size = CHUNKS[c]
        mid, low, high = (begin * unit + size * unit // 2), begin * unit, (begin + size) * unit
        if count == seqs * DRAFT:
            half = count // 2
            return (slice(0, half), slice(low, high)), (slice(half, count), slice(low, high))
        lines = slice(row, row + count)
        return (lines, slice(low, mid)), (lines, slice(mid, high))

    def copies(c):
        kind, lines, cols = area(c)
        if kind == 1:
            pairs = {
                FAR_UP: (part.at[0, 2, lines, cols], far_up.at[lines, cols], up),
                FAR_DOWN: (part.at[1, 2, lines, cols], far_down.at[lines, cols], down),
                NEAR_UP: (part.at[1, 1, lines, cols], from_down.at[1, lines, cols], up),
                NEAR_DOWN: (part.at[0, 3, lines, cols], from_up.at[0, lines, cols], down),
                SUM_UP: (part.at[0, 1, lines, cols], from_down.at[0, lines, cols], up),
                SUM_DOWN: (part.at[1, 3, lines, cols], from_up.at[1, lines, cols], down),
                ACROSS: (part.at[1, 0, lines, cols], across.at[0, lines, cols], over),
            }
        else:
            one, two = halves(c)
            pairs = {
                FAR_UP: (part.at[0, 2, *one], far_up.at[*one], up),
                FAR_DOWN: (part.at[0, 2, *two], far_down.at[*two], down),
                NEAR_UP: (part.at[0, 1, *two], from_down.at[0, *two], up),
                NEAR_DOWN: (part.at[0, 3, *one], from_up.at[0, *one], down),
                SUM_UP: (part.at[0, 1, *one], from_down.at[0, *one], up),
                SUM_DOWN: (part.at[0, 3, *two], from_up.at[0, *two], down),
                ACROSS: (part.at[1, :, lines, cols], across.at[:, lines, cols], over),
            }

        def build(which):
            source, target, device = pairs[which]
            return pltpu.make_async_remote_copy(
                source,
                target,
                r_send.at[c, which],
                r_recv.at[c, which],
                device_id=device,
                device_id_type=MESH,
            )

        return build

    def add(target, *terms):
        value = part[target].astype(F32)
        for ref, index in terms:
            value = value + ref[index].astype(F32)
        part[target] = value.astype(BF16)

    arrived, loaded = set(), set()
    squares = [0.0] * seqs

    def product(c):
        kind, row, count, begin, size = CHUNKS[c]
        for s in range(row // DRAFT, (row + count) // DRAFT):
            if s not in arrived:
                arrived.add(s)
                with jax.named_scope(f"rows#s={s}"):
                    for i in range(KV_HEADS - 1):
                        att_copy(s, i).wait_recv()
        for j, (first, extent) in enumerate(PIECES):
            if j not in loaded and first < begin + size and begin < first + extent:
                loaded.add(j)
                with jax.named_scope(f"weights#j={j}"):
                    w_copy(j).wait()
                    swap_copy(j).wait_recv()

        def tile(n, carry):
            cols = pl.ds(pl.multiple_of(begin * unit + n * TILE, TILE), TILE)
            half = w.shape[1]
            own = pl.ds(pl.multiple_of(core * half, half), half)
            other = pl.ds(pl.multiple_of((1 - core) * half, half), half)
            lines = slice(row, row + count)
            out = jnp.dot(
                att[:, :, lines, own].reshape(8 * count, half),
                w[0, :, cols],
                preferred_element_type=F32,
            ) + jnp.dot(
                att[:, :, lines, other].reshape(8 * count, half),
                w[1, :, cols],
                preferred_element_type=F32,
            )
            part[:, :, lines, cols] = out.astype(BF16).reshape(2, 4, count, TILE)
            return carry

        lax.fori_loop(0, size * unit // TILE, tile, 0)

    def finish(c):
        kind, lines, cols = area(c)
        value = (
            part[0, 0, lines, cols].astype(F32)
            + from_down[0, lines, cols].astype(F32)
            + from_up[0, lines, cols].astype(F32)
            + across[0, lines, cols].astype(F32)
        )
        for n, s in enumerate(range(lines.start // DRAFT, lines.stop // DRAFT)):
            here = value[n * DRAFT : (n + 1) * DRAFT] + res[s, :, cols].astype(F32)
            (total_0, total_1)[s][:, cols] = here
            hid[s, :, cols] = here.astype(BF16)
            squares[s] = squares[s] + jnp.sum(here * here, axis=-1, keepdims=True)

    def advance(step, c):
        kind, lines, cols = area(c)
        build = copies(c)
        every = slice(None)
        if step == "m":
            product(c)
        elif step == "x":
            build(FAR_UP).start()
            build(FAR_DOWN).start()
        elif step == "e":
            build(NEAR_UP).start()
            build(NEAR_DOWN).start()
        elif step == "y":
            build(ACROSS).start()
        elif step == "s":
            build(ACROSS).wait_recv()
            add((0, 2, lines, cols), (across, (2, lines, cols)))
            build(FAR_UP).start()
            build(FAR_DOWN).start()
            for dx in (1, 3):
                add((0, dx, lines, cols), (across, (dx, lines, cols)))
        elif step == "d":
            one, two = halves(c) if kind == 2 else ((lines, cols), (lines, cols))
            build(FAR_UP).wait_recv()
            add((0, 1, *one), (far_up, one))
            build(SUM_UP).start()
            build(FAR_DOWN).wait_recv()
            add((0 if kind == 2 else 1, 3, *two), (far_down, two))
            build(SUM_DOWN).start()
        elif step == "z":
            for which in (NEAR_UP, NEAR_DOWN, SUM_UP, SUM_DOWN):
                build(which).wait_recv()
            add((1, 0, lines, cols), (from_down, (1, lines, cols)), (from_up, (1, lines, cols)))
            build(ACROSS).start()
        else:
            waits = (ACROSS,) if kind == 1 else (NEAR_UP, NEAR_DOWN, SUM_UP, SUM_DOWN)
            for which in waits:
                build(which).wait_recv()
            finish(c)

    res_copy.wait()
    for step, c in PLAN:
        with jax.named_scope(f"{step}#c={c}"):
            advance(step, c)

    with jax.named_scope("scale"):
        for s in range(seqs):
            lane = lax.rsqrt(squares[s] / width + 1e-5)
            scale[s * DRAFT : (s + 1) * DRAFT, :] = jnp.broadcast_to(lane, (DRAFT, 128))

    with jax.named_scope("drain"):
        for s in range(seqs):
            for i in range(KV_HEADS - 1):
                att_copy(s, i).wait_send()
        for j in range(len(PIECES)):
            swap_copy(j).wait_send()
        for c in range(len(CHUNKS)):
            for which in range(7):
                copies(c)(which).wait_send()


def norm_kernel(hid, total_0, total_1, scale, gain, hid_hbm, norm_hbm, norm, sems):
    hid_copy = pltpu.make_async_copy(hid, hid_hbm, sems.at[0])
    hid_copy.start()
    seqs, width = norm.shape[0], norm.shape[2]
    pieces = 4
    size = width // pieces

    def norm_copy(n):
        cols = pl.ds(n * size, size)
        return pltpu.make_async_copy(
            norm.at[:, :, cols], norm_hbm.at[:, :, cols], sems.at[1 + n]
        )

    for n in range(pieces):
        cols = slice(n * size, (n + 1) * size)
        gains = gain[cols].astype(F32).reshape(1, size)
        for s, total in enumerate((total_0, total_1)):
            lane = scale[s * DRAFT : (s + 1) * DRAFT, 0:1]
            norm[s, :, cols] = (total[:, cols] * lane * gains).astype(BF16)
        norm_copy(n).start()
    hid_copy.wait()
    for n in range(pieces):
        norm_copy(n).wait()


def solution(mesh):
    dp_half = mesh.shape["dp"] // 2

    def on_device(queries, kv_cache, lengths, residual, out_weight, norm_gain):
        seqs = queries.shape[0]
        rows = seqs * DRAFT
        depth, width = out_weight.shape
        slots = kv_cache.shape[2]
        chunks, pieces = len(CHUNKS), len(PIECES)
        hbm = pl.BlockSpec(memory_space=pltpu.HBM)
        vmem = pl.BlockSpec(memory_space=pltpu.VMEM)
        dma = pltpu.SemaphoreType.DMA
        sums = pl.pallas_call(
            functools.partial(kernel, dp_half),
            out_shape=(
                jax.ShapeDtypeStruct((seqs, DRAFT, width), BF16),
                jax.ShapeDtypeStruct((DRAFT, width), F32),
                jax.ShapeDtypeStruct((DRAFT, width), F32),
                jax.ShapeDtypeStruct((rows, 128), F32),
            ),
            in_specs=[pl.BlockSpec(memory_space=pltpu.SMEM)] + [hbm] * 4,
            out_specs=(vmem,) * 4,
            scratch_shapes=[
                pltpu.VMEM((seqs, KV_HEADS, DRAFT, GROUP * HEAD_DIM), BF16),
                pltpu.VMEM((seqs, KV_HEADS, slots, 2 * HEAD_DIM), BF16),
                pltpu.VMEM(residual.shape, BF16),
                pltpu.VMEM((2, depth, width), BF16),
                pltpu.VMEM((seqs, KV_HEADS, DRAFT, GROUP * HEAD_DIM), BF16),
                pltpu.VMEM((2, 4, rows, GROUP * HEAD_DIM), BF16),
                pltpu.VMEM((2, 4, rows, width), BF16),
                pltpu.VMEM((rows, width), BF16),
                pltpu.VMEM((rows, width), BF16),
                pltpu.VMEM((2, rows, width), BF16),
                pltpu.VMEM((2, rows, width), BF16),
                pltpu.VMEM((4, rows, width), BF16),
                dma((1,)),
                dma((seqs, KV_HEADS)),
                dma((seqs, KV_HEADS)),
                dma((pieces,)),
                dma((pieces,)),
                dma((pieces,)),
                dma((seqs, KV_HEADS)),
                dma((seqs, KV_HEADS)),
                dma((chunks, 7)),
                dma((chunks, 7)),
            ],
            compiler_params=pltpu.CompilerParams(
                collective_id=0, has_side_effects=True, vmem_limit_bytes=VMEM_LIMIT
            ),
        )(lengths, queries, kv_cache, residual, out_weight)
        return pl.pallas_call(
            norm_kernel,
            out_shape=(jax.ShapeDtypeStruct((seqs, DRAFT, width), BF16),) * 2,
            in_specs=[vmem] * 5,
            out_specs=(hbm, hbm),
            scratch_shapes=[pltpu.VMEM((seqs, DRAFT, width), BF16), dma((5,))],
            compiler_params=pltpu.CompilerParams(vmem_limit_bytes=4 * 1024 * 1024),
        )(*sums, norm_gain)

    seq = P(("dp", "tp"))
    return jax.shard_map(
        on_device,
        mesh=mesh,
        in_specs=(seq, seq, seq, seq, P("tp"), P()),
        out_specs=(seq, seq),
        check_vma=False,
    )
```

time: 168 us -> 47.5 us (0.28); the launches traced: 165 us -> 47.3 us
  waiting for transfers between devices: 106 us -> 0 us
  Pallas kernels: 0 us -> 46 us
  blocking collectives: 22.8 us -> 0 us
  between operations: 14.1 us -> 0.66 us
  matrix products: 12.9 us -> 0 us
  other arithmetic: 5.95 us -> 0 us
  local copies, waits for them, and re-layouts: 3.51 us -> 0.66 us
    reduce_scatter x1 -> x0, waiting for transfers between devices: 106 us -> none  [on_device(): lax.psum_scatter(jnp.dot(flat_rows, out_weight, preferred_element_type=jn...]
    pallas_call x0 -> x2, Pallas kernels: none -> 46 us  [the longest x1 45 us: on_device(): pl.pallas_call(functools.partial(kernel, dp_half), out_shape=(jax.ShapeDt...]
    all_to_all x2 -> x0, blocking collectives: 22.8 us -> none  [turned_blocks(): lax.all_to_all(tiles, axes[k], split_axis=k, concat_axis=k, tiled=True)]
    dot_general x3 -> x0, matrix products: 12.9 us -> none  [the longest x1 10.1 us: on_device(): jnp.dot(flat_rows, out_weight, preferred_element_type=jnp.float32)]
    convert_element_type x2 -> x0, other arithmetic: 2.22 us -> none  [the longest x1 2.22 us: on_device(): (summed * scales * norm_gain.astype(jnp.float32)).astype(jnp.bfloat16)]
  transfers between devices with their start and end apart: 1 -> 0, of which waited for: 1 -> 0; matrix products, arithmetic and copies ran while one was open for 0% -> 0% of each run, Pallas kernels for 0% -> 0%
where the time goes in v2:
time: 47.5 us; the launch traced here: 47.3 us
  Pallas kernels  46 us (97%)
  local copies, waits for them, and re-layouts  0.66 us (1%)
  between operations  0.66 us (1%)
    pallas_call x1, Pallas kernels, on_device(): pl.pallas_call(functools.partial(kernel, dp_half), out_shape=(jax.ShapeDt...  45 us
    pallas_call x1, Pallas kernels, on_device(): pl.pallas_call(norm_kernel, out_shape=(jax.ShapeDtypeStruct((seqs, DRAFT,...  1 us

profile of v2, /device:TPU:192, one launch (start us, length us, event | category | flops | bytes accessed | tf_op | source)
XLA Modules:
  0.0 47.3 jit_solution(13641345299293571855)
XLA Ops:
  0.6 0.0 copy-start
  0.6 0.0 copy-start.1
  0.7 0.7 %copy-done.1 = s32[2]{0:T(128)S(1)} copy-done((s32[2]{0:T(128)S(1)}, s32[2]{0:T(128)}, u32[]{:S(2)}) %copy-start.1) | copy-done | bytes 32
  1.3 45.0 %shard_map.77 = (bf16[2,16,8192]{2,1,0:T(8,128)(2,1)S(1)}, f32[16,8192]{1,0:T(8,128)S(1)}, f32[16,8192]{1,0:T(8,128)S(1)}, f32[32,128]{1,0:T(8,128)S(1)}) custom-call(s32[2]{0:T(128)S(1)} %copy-done.1, bf16[2,16,8192]{2,1,0:T(8,128)(2,1)} %q_hbm.1, bf16[2,8,384,256]{3,2,1,0:T(8,128)(2,1)} %kv_hbm.1, bf16[2,16,8192]{2,1,0:T(8,128)(2,1)} %res_hbm.1, ...), custom_call_target="tpu_custom_call" | custom-call | tf_op jit(solution)/shard_map/pallas_call | solution.py:422
  46.3 0.0 copy-done
  46.3 1.0 %shard_map.78 = (bf16[2,16,8192]{2,1,0:T(8,128)(2,1)}, bf16[2,16,8192]{2,1,0:T(8,128)(2,1)}) custom-call(bf16[2,16,8192]{2,1,0:T(8,128)(2,1)S(1)} %get-tuple-element.6.hid, f32[16,8192]{1,0:T(8,128)S(1)} %get-tuple-element.7.total_0, f32[16,8192]{1,0:T(8,128)S(1)} %get-tuple-element.8.total_1, f32[32,128]{1,0:T(8,128)S(1)} %get-tuple-element.9.scale, ...), custom_call_target="tpu_custom_call" | custom-call | tf_op jit(solution)/shard_map/pallas_call | solution.py:460
Async XLA Ops:
  0.6 45.7 %copy-start = (bf16[8192]{0:T(1024)(128)(2,1)S(1)}, bf16[8192]{0:T(1024)(128)(2,1)}, u32[]{:S(2)}) copy-start(bf16[8192]{0:T(1024)(128)(2,1)} %gain.1) | copy-start | bytes 49156
  0.6 0.7 %copy-start.1 = (s32[2]{0:T(128)S(1)}, s32[2]{0:T(128)}, u32[]{:S(2)}) copy-start(s32[2]{0:T(128)} %lengths.1) | copy-start | bytes 28

commit v3 on v2

--- a/solution.py
+++ b/solution.py
@@ -26,30 +26,34 @@
     (1, 16, 16, 2, 2),
     (2, 0, 32, 11, 2),
     (1, 0, 32, 4, 2),
-    (2, 0, 32, 13, 2),
+    (2, 0, 32, 13, 1),
     (1, 0, 32, 6, 2),
     (1, 0, 32, 8, 1),
+    (2, 0, 32, 14, 1),
     (2, 0, 32, 15, 1),
 )
-PIECES = ((0, 2), (9, 2), (2, 2), (11, 2), (4, 2), (13, 2), (6, 2), (15, 1), (8, 1))
+PIECES = ((0, 2), (9, 2), (2, 2), (11, 2), (4, 2), (13, 1), (6, 2), (14, 1), (8, 1), (15, 1))
 
 FAR_UP, FAR_DOWN, NEAR_UP, NEAR_DOWN, SUM_UP, SUM_DOWN, ACROSS = range(7)
+FAR, SUMS, OVER = range(3)
+ARRIVAL = (FAR, FAR, SUMS, SUMS, SUMS, SUMS, OVER)
 
 PLAN = (
-    ("m", 0), ("x", 0), ("m", 1), ("y", 1), ("e", 0), ("m", 4), ("x", 4), ("e", 4), ("m", 3),
-    ("y", 3), ("d", 0), ("m", 5), ("e", 5), ("x", 5), ("m", 2), ("e", 2), ("m", 6), ("s", 1),
-    ("x", 2), ("y", 6), ("d", 4), ("m", 7), ("x", 7), ("e", 7), ("m", 8), ("y", 8), ("d", 5),
-    ("z", 0), ("m", 9), ("x", 9), ("m", 11), ("y", 11), ("d", 7), ("e", 9), ("m", 10), ("d", 9),
-    ("x", 10), ("d", 1), ("d", 2), ("s", 3), ("e", 1), ("e", 10), ("z", 7), ("z", 5), ("s", 6),
-    ("d", 10), ("s", 8), ("e", 8), ("d", 3), ("z", 4), ("z", 9), ("s", 11), ("z", 2), ("f", 1),
-    ("e", 3), ("e", 6), ("z", 10), ("d", 6), ("d", 8), ("e", 11), ("f", 5), ("d", 11), ("f", 9),
-    ("f", 6), ("f", 7), ("f", 2), ("f", 4), ("f", 8), ("f", 3), ("f", 10), ("f", 0), ("f", 11),
+    ("m", 0), ("x", 0), ("e", 0), ("m", 1), ("y", 1), ("m", 4), ("e", 4), ("x", 4), ("m", 3),
+    ("y", 3), ("d", 0), ("m", 5), ("x", 5), ("e", 5), ("m", 2), ("e", 2), ("x", 2), ("m", 7),
+    ("e", 7), ("m", 8), ("y", 8), ("s", 1), ("m", 6), ("m", 9), ("m", 11), ("x", 9), ("d", 2),
+    ("y", 6), ("d", 4), ("x", 7), ("e", 9), ("m", 12), ("y", 12), ("m", 10), ("x", 10),
+    ("e", 10), ("y", 11), ("d", 5), ("s", 3), ("d", 7), ("d", 10), ("d", 9), ("s", 8), ("s", 6),
+    ("s", 12), ("z", 7), ("z", 4), ("s", 11), ("z", 5), ("e", 1), ("e", 12), ("z", 0), ("d", 3),
+    ("e", 3), ("d", 1), ("e", 6), ("z", 10), ("d", 8), ("z", 9), ("e", 8), ("d", 12), ("d", 6),
+    ("e", 11), ("z", 2), ("d", 11), ("f", 0), ("f", 3), ("f", 5), ("f", 4), ("f", 7), ("f", 8),
+    ("f", 10), ("f", 1), ("f", 9), ("f", 6), ("f", 12), ("f", 2), ("f", 11),
 )
 
 
 def kernel(
     dp_half,
-    lengths,
+    lengths_hbm,
     q_hbm,
     kv_hbm,
     res_hbm,
@@ -58,6 +62,7 @@
     total_0,
     total_1,
     scale,
+    lengths,
     q,
     kv,
     res,
@@ -70,12 +75,12 @@
     from_down,
     from_up,
     across,
-    in_sem,
+    len_sem,
+    res_sem,
     q_sem,
     kv_sem,
     w_sem,
-    swap_send,
-    swap_recv,
+    swap_sem,
     a_send,
     a_recv,
     r_send,
@@ -103,13 +108,13 @@
         dx, dy = turn(i)
         return ((y_hi + dy) % 2) * 4 + (x + dx) % 4
 
-    def q_copy(s, i):
+    def q_copy(s, i, group):
         wide = GROUP * HEAD_DIM
         cols = pl.ds(pl.multiple_of(kv_head(i) * wide, wide), wide)
-        return pltpu.make_async_copy(q_hbm.at[s, :, cols], q.at[s, i], q_sem.at[s, i])
-
-    def kv_copy(s, i):
-        return pltpu.make_async_copy(kv_hbm.at[s, kv_head(i)], kv.at[s, i], kv_sem.at[s, i])
+        return pltpu.make_async_copy(q_hbm.at[s, :, cols], q.at[s, i], q_sem.at[s, group])
+
+    def kv_copy(s, i, group):
+        return pltpu.make_async_copy(kv_hbm.at[s, kv_head(i)], kv.at[s, i], kv_sem.at[s, group])
 
     def w_copy(j):
         cols = pl.ds(PIECES[j][0] * unit, PIECES[j][1] * unit)
@@ -120,28 +125,36 @@
         return pltpu.make_async_remote_copy(
             w_hbm.at[:, cols],
             w.at[1, :, cols],
-            swap_send.at[j],
-            swap_recv.at[j],
+            swap_sem,
+            w_sem.at[j],
             device_id=sibling,
             device_id_type=MESH,
         )
+
+    def load_heads(s, count):
+        for i in range(KV_HEADS):
+            q_copy(s, i, i // count).start()
+            kv_copy(s, i, i // count).start()
+
+    def arrive(ref, sem):
+        pltpu.make_async_copy(ref, ref, sem).wait()
 
     barrier = pltpu.get_barrier_semaphore()
     friends = [sibling] + [peer(i % 4, i // 4) for i in range(1, 8)]
     for friend in friends:
         pl.semaphore_signal(barrier, inc=1, device_id=friend, device_id_type=MESH)
-    for i in range(KV_HEADS):
-        q_copy(0, i).start()
-        kv_copy(0, i).start()
-    res_copy = pltpu.make_async_copy(res_hbm, res, in_sem.at[0])
+    len_copy = pltpu.make_async_copy(lengths_hbm, lengths, len_sem)
+    len_copy.start()
+    load_heads(0, 2)
+    res_copy = pltpu.make_async_copy(res_hbm, res, res_sem)
 
     def att_copy(s, i):
         dx, dy = turn(i)
         return pltpu.make_async_remote_copy(
             stage.at[s, i],
             att.at[dy, (4 - dx) % 4, pl.ds(s * DRAFT, DRAFT)],
-            a_send.at[s, i],
-            a_recv.at[s, i],
+            a_send,
+            a_recv.at[s],
             device_id=peer(dx, dy),
             device_id_type=MESH,
         )
@@ -151,10 +164,10 @@
     slot = lax.broadcasted_iota(jnp.int32, (GROUP * DRAFT, slots), 1)
     ahead = slot - draft
 
-    def attend(s, heads):
-        for i in heads:
-            q_copy(s, i).wait()
-            kv_copy(s, i).wait()
+    def attend(s, heads, group):
+        these = pl.ds(heads[0], len(heads))
+        arrive(q.at[s, these], q_sem.at[s, group])
+        arrive(kv.at[s, these], kv_sem.at[s, group])
         for i in heads:
             own = q[s, i]
             grouped = jnp.concatenate(
@@ -177,7 +190,7 @@
     def some_heads(s, count):
         def body(h, carry):
             heads = [count * h + n for n in range(count)]
-            attend(s, heads)
+            attend(s, heads, h)
             for n in range(count - 1):
                 att_copy(s, heads[n]).start()
 
@@ -190,11 +203,10 @@
         return body
 
     with jax.named_scope("heads#s=0a"):
-        attend(0, (0, 1))
+        len_copy.wait()
+        attend(0, (0, 1), 0)
     for s in range(1, seqs):
-        for i in range(KV_HEADS):
-            q_copy(s, i).start()
-            kv_copy(s, i).start()
+        load_heads(s, 4)
     with jax.named_scope("barrier"):
         pl.semaphore_wait(barrier, len(friends))
     for i in (0, 1):
@@ -255,8 +267,8 @@
             return pltpu.make_async_remote_copy(
                 source,
                 target,
-                r_send.at[c, which],
-                r_recv.at[c, which],
+                r_send,
+                r_recv.at[c, ARRIVAL[which]],
                 device_id=device,
                 device_id_type=MESH,
             )
@@ -269,6 +281,12 @@
             value = value + ref[index].astype(F32)
         part[target] = value.astype(BF16)
 
+    def wait_for(c, what):
+        kind, lines, cols = area(c)
+        one, two, four = far_up.at[lines, cols], from_down.at[:, lines, cols], across.at[:, lines, cols]
+        sizes = {FAR: (two, one), SUMS: (four, two), OVER: (one, four)}
+        arrive(sizes[what][kind - 1], r_recv.at[c, what])
+
     arrived, loaded = set(), set()
     squares = [0.0] * seqs
 
@@ -277,15 +295,11 @@
         for s in range(row // DRAFT, (row + count) // DRAFT):
             if s not in arrived:
                 arrived.add(s)
-                with jax.named_scope(f"rows#s={s}"):
-                    for i in range(KV_HEADS - 1):
-                        att_copy(s, i).wait_recv()
+                arrive(stage.at[s, : KV_HEADS - 1], a_recv.at[s])
         for j, (first, extent) in enumerate(PIECES):
             if j not in loaded and first < begin + size and begin < first + extent:
                 loaded.add(j)
-                with jax.named_scope(f"weights#j={j}"):
-                    w_copy(j).wait()
-                    swap_copy(j).wait_recv()
+                arrive(w.at[:, :, first * unit : (first + extent) * unit], w_sem.at[j])
 
         def tile(n, carry):
             cols = pl.ds(pl.multiple_of(begin * unit + n * TILE, TILE), TILE)
@@ -336,7 +350,7 @@
         elif step == "y":
             build(ACROSS).start()
         elif step == "s":
-            build(ACROSS).wait_recv()
+            wait_for(c, OVER)
             add((0, 2, lines, cols), (across, (2, lines, cols)))
             build(FAR_UP).start()
             build(FAR_DOWN).start()
@@ -344,21 +358,17 @@
                 add((0, dx, lines, cols), (across, (dx, lines, cols)))
         elif step == "d":
             one, two = halves(c) if kind == 2 else ((lines, cols), (lines, cols))
-            build(FAR_UP).wait_recv()
+            wait_for(c, FAR)
             add((0, 1, *one), (far_up, one))
             build(SUM_UP).start()
-            build(FAR_DOWN).wait_recv()
             add((0 if kind == 2 else 1, 3, *two), (far_down, two))
             build(SUM_DOWN).start()
         elif step == "z":
-            for which in (NEAR_UP, NEAR_DOWN, SUM_UP, SUM_DOWN):
-                build(which).wait_recv()
+            wait_for(c, SUMS)
             add((1, 0, lines, cols), (from_down, (1, lines, cols)), (from_up, (1, lines, cols)))
             build(ACROSS).start()
         else:
-            waits = (ACROSS,) if kind == 1 else (NEAR_UP, NEAR_DOWN, SUM_UP, SUM_DOWN)
-            for which in waits:
-                build(which).wait_recv()
+            wait_for(c, OVER if kind == 1 else SUMS)
             finish(c)
 
     res_copy.wait()
@@ -372,14 +382,12 @@
             scale[s * DRAFT : (s + 1) * DRAFT, :] = jnp.broadcast_to(lane, (DRAFT, 128))
 
     with jax.named_scope("drain"):
-        for s in range(seqs):
-            for i in range(KV_HEADS - 1):
-                att_copy(s, i).wait_send()
-        for j in range(len(PIECES)):
-            swap_copy(j).wait_send()
-        for c in range(len(CHUNKS)):
-            for which in range(7):
-                copies(c)(which).wait_send()
+        arrive(stage.at[:, : KV_HEADS - 1], a_send)
+        arrive(w.at[0], swap_sem)
+        sent = 0
+        for kind, row, count, begin, size in CHUNKS:
+            sent += (7 * count if kind == 1 else 3 * count + 4 * count) * size * unit
+        arrive(w.at[0, :, : sent // w.shape[1]], r_send)
 
 
 def norm_kernel(hid, total_0, total_1, scale, gain, hid_hbm, norm_hbm, norm, sems):
@@ -427,9 +435,10 @@
                 jax.ShapeDtypeStruct((DRAFT, width), F32),
                 jax.ShapeDtypeStruct((rows, 128), F32),
             ),
-            in_specs=[pl.BlockSpec(memory_space=pltpu.SMEM)] + [hbm] * 4,
+            in_specs=[pl.BlockSpec(memory_space=pl.ANY)] + [hbm] * 4,
             out_specs=(vmem,) * 4,
             scratch_shapes=[
+                pltpu.SMEM((seqs,), jnp.int32),
                 pltpu.VMEM((seqs, KV_HEADS, DRAFT, GROUP * HEAD_DIM), BF16),
                 pltpu.VMEM((seqs, KV_HEADS, slots, 2 * HEAD_DIM), BF16),
                 pltpu.VMEM(residual.shape, BF16),
@@ -442,16 +451,16 @@
                 pltpu.VMEM((2, rows, width), BF16),
                 pltpu.VMEM((2, rows, width), BF16),
                 pltpu.VMEM((4, rows, width), BF16),
-                dma((1,)),
-                dma((seqs, KV_HEADS)),
-                dma((seqs, KV_HEADS)),
+                dma,
+                dma,
+                dma((seqs, KV_HEADS // 2)),
+                dma((seqs, KV_HEADS // 2)),
                 dma((pieces,)),
-                dma((pieces,)),
-                dma((pieces,)),
-                dma((seqs, KV_HEADS)),
-                dma((seqs, KV_HEADS)),
-                dma((chunks, 7)),
-                dma((chunks, 7)),
+                dma,
+                dma,
+                dma((seqs,)),
+                dma,
+                dma((chunks, 3)),
             ],
             compiler_params=pltpu.CompilerParams(
                 collective_id=0, has_side_effects=True, vmem_limit_bytes=VMEM_LIMIT

time: 47.5 us -> 45.5 us (0.958)
  Pallas kernels: 46 us -> 44 us
    pallas_call x1, Pallas kernels: 45 us -> 43 us  [on_device(): pl.pallas_call(functools.partial(kernel, dp_half), out_shape=(jax.ShapeDt...]
where the time goes in v3:
time: 45.5 us; the launch traced here: 45.3 us
  Pallas kernels  44 us (97%)
  local copies, waits for them, and re-layouts  0.66 us (1%)
  between operations  0.66 us (1%)
    pallas_call x1, Pallas kernels, on_device(): pl.pallas_call(functools.partial(kernel, dp_half), out_shape=(jax.ShapeDt...  43 us
    pallas_call x1, Pallas kernels, on_device(): pl.pallas_call(norm_kernel, out_shape=(jax.ShapeDtypeStruct((seqs, DRAFT,...  1 us

profile of v3, /device:TPU:192, one launch (start us, length us, event | category | flops | bytes accessed | tf_op | source)
XLA Modules:
  0.0 45.3 jit_solution(6495556586654391684)
XLA Ops:
  0.6 0.0 copy-start
  0.6 0.0 copy-start.1
  0.7 0.7 %copy-done.1 = s32[2]{0:T(128)S(1)} copy-done((s32[2]{0:T(128)S(1)}, s32[2]{0:T(128)}, u32[]{:S(2)}) %copy-start.1) | copy-done | bytes 32
  1.3 43.0 %shard_map.77 = (bf16[2,16,8192]{2,1,0:T(8,128)(2,1)S(1)}, f32[16,8192]{1,0:T(8,128)S(1)}, f32[16,8192]{1,0:T(8,128)S(1)}, f32[32,128]{1,0:T(8,128)S(1)}) custom-call(s32[2]{0:T(128)S(1)} %copy-done.1, bf16[2,16,8192]{2,1,0:T(8,128)(2,1)} %q_hbm.1, bf16[2,8,384,256]{3,2,1,0:T(8,128)(2,1)} %kv_hbm.1, bf16[2,16,8192]{2,1,0:T(8,128)(2,1)} %res_hbm.1, ...), custom_call_target="tpu_custom_call" | custom-call | tf_op jit(solution)/shard_map/pallas_call | solution.py:430
  44.3 0.0 copy-done
  44.3 1.0 %shard_map.78 = (bf16[2,16,8192]{2,1,0:T(8,128)(2,1)}, bf16[2,16,8192]{2,1,0:T(8,128)(2,1)}) custom-call(bf16[2,16,8192]{2,1,0:T(8,128)(2,1)S(1)} %get-tuple-element.6.hid, f32[16,8192]{1,0:T(8,128)S(1)} %get-tuple-element.7.total_0, f32[16,8192]{1,0:T(8,128)S(1)} %get-tuple-element.8.total_1, f32[32,128]{1,0:T(8,128)S(1)} %get-tuple-element.9.scale, ...), custom_call_target="tpu_custom_call" | custom-call | tf_op jit(solution)/shard_map/pallas_call | solution.py:469
Async XLA Ops:
  0.6 43.7 %copy-start = (bf16[8192]{0:T(1024)(128)(2,1)S(1)}, bf16[8192]{0:T(1024)(128)(2,1)}, u32[]{:S(2)}) copy-start(bf16[8192]{0:T(1024)(128)(2,1)} %gain.1) | copy-start | bytes 49156
  0.6 0.7 %copy-start.1 = (s32[2]{0:T(128)S(1)}, s32[2]{0:T(128)}, u32[]{:S(2)}) copy-start(s32[2]{0:T(128)} %lengths_hbm.1) | copy-start | bytes 28

commit v4 on v3

--- a/solution.py
+++ b/solution.py
@@ -12,7 +12,7 @@
 GROUP = 8
 DRAFT = 16
 TILE = 512
-VMEM_LIMIT = 54735667
+VMEM_LIMIT = 50 * 1024 * 1024
 MESH = pl.DeviceIdType.MESH
 F32 = jnp.float32
 BF16 = jnp.bfloat16
@@ -39,15 +39,15 @@
 ARRIVAL = (FAR, FAR, SUMS, SUMS, SUMS, SUMS, OVER)
 
 PLAN = (
-    ("m", 0), ("x", 0), ("e", 0), ("m", 1), ("y", 1), ("m", 4), ("e", 4), ("x", 4), ("m", 3),
-    ("y", 3), ("d", 0), ("m", 5), ("x", 5), ("e", 5), ("m", 2), ("e", 2), ("x", 2), ("m", 7),
-    ("e", 7), ("m", 8), ("y", 8), ("s", 1), ("m", 6), ("m", 9), ("m", 11), ("x", 9), ("d", 2),
-    ("y", 6), ("d", 4), ("x", 7), ("e", 9), ("m", 12), ("y", 12), ("m", 10), ("x", 10),
-    ("e", 10), ("y", 11), ("d", 5), ("s", 3), ("d", 7), ("d", 10), ("d", 9), ("s", 8), ("s", 6),
-    ("s", 12), ("z", 7), ("z", 4), ("s", 11), ("z", 5), ("e", 1), ("e", 12), ("z", 0), ("d", 3),
-    ("e", 3), ("d", 1), ("e", 6), ("z", 10), ("d", 8), ("z", 9), ("e", 8), ("d", 12), ("d", 6),
-    ("e", 11), ("z", 2), ("d", 11), ("f", 0), ("f", 3), ("f", 5), ("f", 4), ("f", 7), ("f", 8),
-    ("f", 10), ("f", 1), ("f", 9), ("f", 6), ("f", 12), ("f", 2), ("f", 11),
+    ("m", 0), ("x", 0), ("m", 1), ("y", 1), ("e", 0), ("m", 4), ("e", 4), ("x", 4), ("m", 3),
+    ("y", 3), ("d", 0), ("m", 2), ("x", 2), ("e", 2), ("m", 5), ("x", 5), ("m", 8), ("y", 8),
+    ("e", 5), ("m", 7), ("e", 7), ("m", 6), ("y", 6), ("d", 2), ("m", 9), ("x", 7), ("m", 10),
+    ("x", 9), ("e", 10), ("m", 11), ("x", 10), ("s", 8), ("s", 1), ("e", 9), ("y", 11),
+    ("e", 1), ("d", 5), ("s", 3), ("d", 9), ("d", 10), ("d", 4), ("m", 12), ("y", 12), ("d", 7),
+    ("s", 6), ("s", 11), ("z", 9), ("d", 3), ("z", 2), ("z", 0), ("d", 1), ("s", 12), ("d", 8),
+    ("e", 3), ("e", 8), ("z", 7), ("z", 5), ("z", 4), ("d", 11), ("e", 11), ("d", 6), ("e", 6),
+    ("z", 10), ("f", 9), ("e", 12), ("d", 12), ("f", 2), ("f", 0), ("f", 8), ("f", 1), ("f", 7),
+    ("f", 4), ("f", 3), ("f", 5), ("f", 11), ("f", 10), ("f", 6), ("f", 12),
 )
 
 
@@ -427,6 +427,7 @@
         hbm = pl.BlockSpec(memory_space=pltpu.HBM)
         vmem = pl.BlockSpec(memory_space=pltpu.VMEM)
         dma = pltpu.SemaphoreType.DMA
+        in_hbm = functools.partial(pltpu.with_memory_space_constraint, memory_space=pltpu.HBM)
         sums = pl.pallas_call(
             functools.partial(kernel, dp_half),
             out_shape=(
@@ -435,7 +436,7 @@
                 jax.ShapeDtypeStruct((DRAFT, width), F32),
                 jax.ShapeDtypeStruct((rows, 128), F32),
             ),
-            in_specs=[pl.BlockSpec(memory_space=pl.ANY)] + [hbm] * 4,
+            in_specs=[hbm] * 5,
             out_specs=(vmem,) * 4,
             scratch_shapes=[
                 pltpu.SMEM((seqs,), jnp.int32),
@@ -465,7 +466,7 @@
             compiler_params=pltpu.CompilerParams(
                 collective_id=0, has_side_effects=True, vmem_limit_bytes=VMEM_LIMIT
             ),
-        )(lengths, queries, kv_cache, residual, out_weight)
+        )(*(in_hbm(a) for a in (lengths, queries, kv_cache, residual, out_weight)))
         return pl.pallas_call(
             norm_kernel,
             out_shape=(jax.ShapeDtypeStruct((seqs, DRAFT, width), BF16),) * 2,

time: 45.5 us -> 44.7 us (0.982)
  local copies, waits for them, and re-layouts: 0.66 us -> 0.01 us
    unnamed x4 -> x2, local copies, waits for them, and re-layouts: 0.66 us -> 0.01 us
where the time goes in v4:
time: 44.7 us; the launch traced here: 44.6 us
  Pallas kernels  43.9 us (98%)
  between operations  0.66 us (1%)
    pallas_call x1, Pallas kernels, on_device(): pl.pallas_call(functools.partial(kernel, dp_half), out_shape=(jax.ShapeDt...  42.9 us
    pallas_call x1, Pallas kernels, on_device(): pl.pallas_call(norm_kernel, out_shape=(jax.ShapeDtypeStruct((seqs, DRAFT,...  1 us

profile of v4, /device:TPU:192, one launch (start us, length us, event | category | flops | bytes accessed | tf_op | source)
XLA Modules:
  0.0 44.6 jit_solution(12209486685428352650)
XLA Ops:
  0.6 0.0 copy-start
  0.6 42.9 %shard_map.77 = (bf16[2,16,8192]{2,1,0:T(8,128)(2,1)S(1)}, f32[16,8192]{1,0:T(8,128)S(1)}, f32[16,8192]{1,0:T(8,128)S(1)}, f32[32,128]{1,0:T(8,128)S(1)}) custom-call(s32[2]{0:T(128)} %lengths_hbm.1, bf16[2,16,8192]{2,1,0:T(8,128)(2,1)} %q_hbm.1, bf16[2,8,384,256]{3,2,1,0:T(8,128)(2,1)} %kv_hbm.1, bf16[2,16,8192]{2,1,0:T(8,128)(2,1)} %res_hbm.1, ...), custom_call_target="tpu_custom_call" | custom-call | tf_op jit(solution)/shard_map/pallas_call | solution.py:431
  43.6 0.0 copy-done
  43.6 1.0 %shard_map.78 = (bf16[2,16,8192]{2,1,0:T(8,128)(2,1)}, bf16[2,16,8192]{2,1,0:T(8,128)(2,1)}) custom-call(bf16[2,16,8192]{2,1,0:T(8,128)(2,1)S(1)} %get-tuple-element.6.hid, f32[16,8192]{1,0:T(8,128)S(1)} %get-tuple-element.7.total_0, f32[16,8192]{1,0:T(8,128)S(1)} %get-tuple-element.8.total_1, f32[32,128]{1,0:T(8,128)S(1)} %get-tuple-element.9.scale, ...), custom_call_target="tpu_custom_call" | custom-call | tf_op jit(solution)/shard_map/pallas_call | solution.py:470
Async XLA Ops:
  0.6 42.9 %copy-start = (bf16[8192]{0:T(1024)(128)(2,1)S(1)}, bf16[8192]{0:T(1024)(128)(2,1)}, u32[]{:S(2)}) copy-start(bf16[8192]{0:T(1024)(128)(2,1)} %gain.1) | copy-start | bytes 49156

commit v5 on v4

--- a/solution.py
+++ b/solution.py
@@ -38,16 +38,27 @@
 FAR, SUMS, OVER = range(3)
 ARRIVAL = (FAR, FAR, SUMS, SUMS, SUMS, SUMS, OVER)
 
-PLAN = (
+PLAN_0 = (
+    ("m", 0), ("e", 0), ("m", 1), ("x", 0), ("y", 1), ("m", 4), ("e", 4), ("x", 4), ("m", 5),
+    ("x", 5), ("e", 5), ("m", 6), ("y", 6), ("m", 2), ("x", 2), ("d", 0), ("m", 7), ("x", 7),
+    ("e", 7), ("m", 3), ("y", 3), ("m", 9), ("m", 11), ("m", 10), ("d", 4), ("s", 1), ("e", 9),
+    ("e", 10), ("m", 8), ("x", 10), ("x", 9), ("y", 11), ("d", 5), ("z", 0), ("y", 8),
+    ("m", 12), ("y", 12), ("s", 6), ("d", 7), ("e", 2), ("d", 2), ("s", 11), ("s", 8), ("d", 9),
+    ("d", 10), ("s", 3), ("f", 0), ("z", 5), ("s", 12), ("d", 6), ("e", 12), ("e", 11),
+    ("d", 8), ("z", 7), ("d", 1), ("e", 3), ("z", 2), ("e", 8), ("d", 11), ("e", 6), ("z", 10),
+    ("d", 3), ("e", 1), ("z", 4), ("d", 12), ("z", 9), ("f", 4), ("f", 6), ("f", 10), ("f", 5),
+    ("f", 2), ("f", 8), ("f", 3), ("f", 11), ("f", 7), ("f", 1), ("f", 12), ("f", 9),
+)
+PLAN_1 = (
     ("m", 0), ("x", 0), ("m", 1), ("y", 1), ("e", 0), ("m", 4), ("e", 4), ("x", 4), ("m", 3),
-    ("y", 3), ("d", 0), ("m", 2), ("x", 2), ("e", 2), ("m", 5), ("x", 5), ("m", 8), ("y", 8),
-    ("e", 5), ("m", 7), ("e", 7), ("m", 6), ("y", 6), ("d", 2), ("m", 9), ("x", 7), ("m", 10),
-    ("x", 9), ("e", 10), ("m", 11), ("x", 10), ("s", 8), ("s", 1), ("e", 9), ("y", 11),
-    ("e", 1), ("d", 5), ("s", 3), ("d", 9), ("d", 10), ("d", 4), ("m", 12), ("y", 12), ("d", 7),
-    ("s", 6), ("s", 11), ("z", 9), ("d", 3), ("z", 2), ("z", 0), ("d", 1), ("s", 12), ("d", 8),
-    ("e", 3), ("e", 8), ("z", 7), ("z", 5), ("z", 4), ("d", 11), ("e", 11), ("d", 6), ("e", 6),
-    ("z", 10), ("f", 9), ("e", 12), ("d", 12), ("f", 2), ("f", 0), ("f", 8), ("f", 1), ("f", 7),
-    ("f", 4), ("f", 3), ("f", 5), ("f", 11), ("f", 10), ("f", 6), ("f", 12),
+    ("d", 0), ("y", 3), ("m", 2), ("e", 2), ("x", 2), ("m", 5), ("x", 5), ("m", 7), ("x", 7),
+    ("s", 1), ("m", 9), ("m", 11), ("e", 9), ("x", 9), ("m", 8), ("d", 5), ("y", 8), ("d", 4),
+    ("s", 3), ("e", 7), ("m", 12), ("d", 2), ("d", 9), ("m", 10), ("m", 6), ("y", 6), ("e", 5),
+    ("s", 8), ("y", 11), ("x", 10), ("y", 12), ("d", 10), ("e", 10), ("d", 7), ("s", 6),
+    ("z", 9), ("s", 11), ("s", 12), ("d", 8), ("e", 6), ("e", 3), ("z", 2), ("d", 1), ("z", 0),
+    ("e", 11), ("z", 5), ("z", 10), ("d", 3), ("z", 7), ("e", 1), ("e", 8), ("z", 4), ("d", 6),
+    ("d", 11), ("e", 12), ("f", 9), ("d", 12), ("f", 2), ("f", 10), ("f", 5), ("f", 0),
+    ("f", 8), ("f", 1), ("f", 3), ("f", 6), ("f", 11), ("f", 7), ("f", 4), ("f", 12),
 )
 
 
@@ -131,10 +142,11 @@
             device_id_type=MESH,
         )
 
-    def load_heads(s, count):
-        for i in range(KV_HEADS):
-            q_copy(s, i, i // count).start()
-            kv_copy(s, i, i // count).start()
+    def load_heads(s, groups):
+        for group, heads in enumerate(groups):
+            for i in heads:
+                q_copy(s, i, group).start()
+                kv_copy(s, i, group).start()
 
     def arrive(ref, sem):
         pltpu.make_async_copy(ref, ref, sem).wait()
@@ -145,7 +157,7 @@
         pl.semaphore_signal(barrier, inc=1, device_id=friend, device_id_type=MESH)
     len_copy = pltpu.make_async_copy(lengths_hbm, lengths, len_sem)
     len_copy.start()
-    load_heads(0, 2)
+    load_heads(0, ((0, 1), (2, 3), (4, 5), (6, 7)))
     res_copy = pltpu.make_async_copy(res_hbm, res, res_sem)
 
     def att_copy(s, i):
@@ -206,7 +218,7 @@
         len_copy.wait()
         attend(0, (0, 1), 0)
     for s in range(1, seqs):
-        load_heads(s, 4)
+        load_heads(s, ((0, 1), (2, 3), (4, 5, 6, 7)))
     with jax.named_scope("barrier"):
         pl.semaphore_wait(barrier, len(friends))
     for i in (0, 1):
@@ -219,7 +231,10 @@
         lax.fori_loop(1, KV_HEADS // 2, some_heads(0, 2), 0)
     for s in range(1, seqs):
         with jax.named_scope("heads#s=1"):
-            lax.fori_loop(0, KV_HEADS // 4, some_heads(s, 4), 0)
+            lax.fori_loop(0, 2, some_heads(s, 2), 0)
+            attend(s, (4, 5, 6, 7), 2)
+            for i in (4, 5, 6):
+                att_copy(s, i).start()
     for s in range(seqs):
         att[0, 0, s * DRAFT : (s + 1) * DRAFT] = stage[s, KV_HEADS - 1]
 
@@ -287,99 +302,108 @@
         sizes = {FAR: (two, one), SUMS: (four, two), OVER: (one, four)}
         arrive(sizes[what][kind - 1], r_recv.at[c, what])
 
-    arrived, loaded = set(), set()
-    squares = [0.0] * seqs
-
-    def product(c):
-        kind, row, count, begin, size = CHUNKS[c]
-        for s in range(row // DRAFT, (row + count) // DRAFT):
-            if s not in arrived:
-                arrived.add(s)
-                arrive(stage.at[s, : KV_HEADS - 1], a_recv.at[s])
-        for j, (first, extent) in enumerate(PIECES):
-            if j not in loaded and first < begin + size and begin < first + extent:
-                loaded.add(j)
-                arrive(w.at[:, :, first * unit : (first + extent) * unit], w_sem.at[j])
-
-        def tile(n, carry):
-            cols = pl.ds(pl.multiple_of(begin * unit + n * TILE, TILE), TILE)
-            half = w.shape[1]
-            own = pl.ds(pl.multiple_of(core * half, half), half)
-            other = pl.ds(pl.multiple_of((1 - core) * half, half), half)
-            lines = slice(row, row + count)
-            out = jnp.dot(
-                att[:, :, lines, own].reshape(8 * count, half),
-                w[0, :, cols],
-                preferred_element_type=F32,
-            ) + jnp.dot(
-                att[:, :, lines, other].reshape(8 * count, half),
-                w[1, :, cols],
-                preferred_element_type=F32,
+    def run(plan):
+        arrived, loaded = set(), set()
+        squares = [0.0] * seqs
+
+        def product(c):
+            kind, row, count, begin, size = CHUNKS[c]
+            for s in range(row // DRAFT, (row + count) // DRAFT):
+                if s not in arrived:
+                    arrived.add(s)
+                    arrive(stage.at[s, : KV_HEADS - 1], a_recv.at[s])
+            for j, (first, extent) in enumerate(PIECES):
+                if j not in loaded and first < begin + size and begin < first + extent:
+                    loaded.add(j)
+                    arrive(w.at[:, :, first * unit : (first + extent) * unit], w_sem.at[j])
+
+            def tile(n, carry):
+                cols = pl.ds(pl.multiple_of(begin * unit + n * TILE, TILE), TILE)
+                half = w.shape[1]
+                own = pl.ds(pl.multiple_of(core * half, half), half)
+                other = pl.ds(pl.multiple_of((1 - core) * half, half), half)
+                lines = slice(row, row + count)
+                out = jnp.dot(
+                    att[:, :, lines, own].reshape(8 * count, half),
+                    w[0, :, cols],
+                    preferred_element_type=F32,
+                ) + jnp.dot(
+                    att[:, :, lines, other].reshape(8 * count, half),
+                    w[1, :, cols],
+                    preferred_element_type=F32,
+                )
+                part[:, :, lines, cols] = out.astype(BF16).reshape(2, 4, count, TILE)
+                return carry
+
+            lax.fori_loop(0, size * unit // TILE, tile, 0)
+
+        def finish(c):
+            kind, lines, cols = area(c)
+            value = (
+                part[0, 0, lines, cols].astype(F32)
+                + from_down[0, lines, cols].astype(F32)
+                + from_up[0, lines, cols].astype(F32)
+                + across[0, lines, cols].astype(F32)
             )
-            part[:, :, lines, cols] = out.astype(BF16).reshape(2, 4, count, TILE)
-            return carry
-
-        lax.fori_loop(0, size * unit // TILE, tile, 0)
-
-    def finish(c):
-        kind, lines, cols = area(c)
-        value = (
-            part[0, 0, lines, cols].astype(F32)
-            + from_down[0, lines, cols].astype(F32)
-            + from_up[0, lines, cols].astype(F32)
-            + across[0, lines, cols].astype(F32)
-        )
-        for n, s in enumerate(range(lines.start // DRAFT, lines.stop // DRAFT)):
-            here = value[n * DRAFT : (n + 1) * DRAFT] + res[s, :, cols].astype(F32)
-            (total_0, total_1)[s][:, cols] = here
-            hid[s, :, cols] = here.astype(BF16)
-            squares[s] = squares[s] + jnp.sum(here * here, axis=-1, keepdims=True)
-
-    def advance(step, c):
-        kind, lines, cols = area(c)
-        build = copies(c)
-        every = slice(None)
-        if step == "m":
-            product(c)
-        elif step == "x":
-            build(FAR_UP).start()
-            build(FAR_DOWN).start()
-        elif step == "e":
-            build(NEAR_UP).start()
-            build(NEAR_DOWN).start()
-        elif step == "y":
-            build(ACROSS).start()
-        elif step == "s":
-            wait_for(c, OVER)
-            add((0, 2, lines, cols), (across, (2, lines, cols)))
-            build(FAR_UP).start()
-            build(FAR_DOWN).start()
-            for dx in (1, 3):
-                add((0, dx, lines, cols), (across, (dx, lines, cols)))
-        elif step == "d":
-            one, two = halves(c) if kind == 2 else ((lines, cols), (lines, cols))
-            wait_for(c, FAR)
-            add((0, 1, *one), (far_up, one))
-            build(SUM_UP).start()
-            add((0 if kind == 2 else 1, 3, *two), (far_down, two))
-            build(SUM_DOWN).start()
-        elif step == "z":
-            wait_for(c, SUMS)
-            add((1, 0, lines, cols), (from_down, (1, lines, cols)), (from_up, (1, lines, cols)))
-            build(ACROSS).start()
-        else:
-            wait_for(c, OVER if kind == 1 else SUMS)
-            finish(c)
-
-    res_copy.wait()
-    for step, c in PLAN:
-        with jax.named_scope(f"{step}#c={c}"):
-            advance(step, c)
-
-    with jax.named_scope("scale"):
-        for s in range(seqs):
-            lane = lax.rsqrt(squares[s] / width + 1e-5)
-            scale[s * DRAFT : (s + 1) * DRAFT, :] = jnp.broadcast_to(lane, (DRAFT, 128))
+            for n, s in enumerate(range(lines.start // DRAFT, lines.stop // DRAFT)):
+                here = value[n * DRAFT : (n + 1) * DRAFT] + res[s, :, cols].astype(F32)
+                (total_0, total_1)[s][:, cols] = here
+                hid[s, :, cols] = here.astype(BF16)
+                squares[s] = squares[s] + jnp.sum(here * here, axis=-1, keepdims=True)
+
+        def advance(step, c):
+            kind, lines, cols = area(c)
+            build = copies(c)
+            every = slice(None)
+            if step == "m":
+                product(c)
+            elif step == "x":
+                build(FAR_UP).start()
+                build(FAR_DOWN).start()
+            elif step == "e":
+                build(NEAR_UP).start()
+                build(NEAR_DOWN).start()
+            elif step == "y":
+                build(ACROSS).start()
+            elif step == "s":
+                wait_for(c, OVER)
+                add((0, 2, lines, cols), (across, (2, lines, cols)))
+                build(FAR_UP).start()
+                build(FAR_DOWN).start()
+                for dx in (1, 3):
+                    add((0, dx, lines, cols), (across, (dx, lines, cols)))
+            elif step == "d":
+                one, two = halves(c) if kind == 2 else ((lines, cols), (lines, cols))
+                wait_for(c, FAR)
+                add((0, 1, *one), (far_up, one))
+                build(SUM_UP).start()
+                add((0 if kind == 2 else 1, 3, *two), (far_down, two))
+                build(SUM_DOWN).start()
+            elif step == "z":
+                wait_for(c, SUMS)
+                add((1, 0, lines, cols), (from_down, (1, lines, cols)), (from_up, (1, lines, cols)))
+                build(ACROSS).start()
+            else:
+                wait_for(c, OVER if kind == 1 else SUMS)
+                finish(c)
+
+        res_copy.wait()
+        for step, c in plan:
+            with jax.named_scope(f"{step}#c={c}"):
+                advance(step, c)
+
+        with jax.named_scope("scale"):
+            for s in range(seqs):
+                lane = lax.rsqrt(squares[s] / width + 1e-5)
+                scale[s * DRAFT : (s + 1) * DRAFT, :] = jnp.broadcast_to(lane, (DRAFT, 128))
+
+    @pl.when(core == 0)
+    def _():
+        run(PLAN_0)
+
+    @pl.when(core == 1)
+    def _():
+        run(PLAN_1)
 
     with jax.named_scope("drain"):
         arrive(stage.at[:, : KV_HEADS - 1], a_send)

time: 44.7 us -> 44.7 us (level)
  the two profiles are of different devices: /device:TPU:192 before, /device:TPU:1 now
where the time goes in v5:
time: 44.7 us; the launch traced here: 44.6 us
  Pallas kernels  43.9 us (98%)
  between operations  0.66 us (1%)
    pallas_call x1, Pallas kernels, on_device(): pl.pallas_call(functools.partial(kernel, dp_half), out_shape=(jax.ShapeDt...  42.9 us
    pallas_call x1, Pallas kernels, on_device(): pl.pallas_call(norm_kernel, out_shape=(jax.ShapeDtypeStruct((seqs, DRAFT,...  1 us

profile of v5, /device:TPU:1, one launch (start us, length us, event | category | flops | bytes accessed | tf_op | source)
XLA Modules:
  0.0 44.6 jit_solution(13995264091390694116)
XLA Ops:
  0.6 0.0 copy-start
  0.6 42.9 %shard_map.77 = (bf16[2,16,8192]{2,1,0:T(8,128)(2,1)S(1)}, f32[16,8192]{1,0:T(8,128)S(1)}, f32[16,8192]{1,0:T(8,128)S(1)}, f32[32,128]{1,0:T(8,128)S(1)}) custom-call(s32[2]{0:T(128)} %lengths_hbm.1, bf16[2,16,8192]{2,1,0:T(8,128)(2,1)} %q_hbm.1, bf16[2,8,384,256]{3,2,1,0:T(8,128)(2,1)} %kv_hbm.1, bf16[2,16,8192]{2,1,0:T(8,128)(2,1)} %res_hbm.1, ...), custom_call_target="tpu_custom_call" | custom-call | tf_op jit(solution)/shard_map/pallas_call | solution.py:455
  43.6 0.0 copy-done
  43.6 1.0 %shard_map.78 = (bf16[2,16,8192]{2,1,0:T(8,128)(2,1)}, bf16[2,16,8192]{2,1,0:T(8,128)(2,1)}) custom-call(bf16[2,16,8192]{2,1,0:T(8,128)(2,1)S(1)} %get-tuple-element.6.hid, f32[16,8192]{1,0:T(8,128)S(1)} %get-tuple-element.7.total_0, f32[16,8192]{1,0:T(8,128)S(1)} %get-tuple-element.8.total_1, f32[32,128]{1,0:T(8,128)S(1)} %get-tuple-element.9.scale, ...), custom_call_target="tpu_custom_call" | custom-call | tf_op jit(solution)/shard_map/pallas_call | solution.py:494
Async XLA Ops:
  0.6 42.9 %copy-start = (bf16[8192]{0:T(1024)(128)(2,1)S(1)}, bf16[8192]{0:T(1024)(128)(2,1)}, u32[]{:S(2)}) copy-start(bf16[8192]{0:T(1024)(128)(2,1)} %gain.1) | copy-start | bytes 49156
